TPU v7x, 128 devices: a whole 4x4x4 slice. The times are simulated.
128 devices in a mesh: fsdp: 32 (over z, x_lo, y), mp: 4 (over x_hi, core).
Axes of the slice: x: 4 (x_hi: 2, x_lo: 2; x = x_hi * 2 + x_lo), y: 4, z: 4, core: 2. Of those that a mesh axis runs over, the one named last changes fastest.
Arguments:
- first_moment: float32 [1, 16, 32, 128, 1024], P(None, None, 'fsdp', 'mp'), may hold values from -20 to 20
- second_moment: float32 [1, 16, 32, 128, 1024], P(None, None, 'fsdp', 'mp'), may hold values from 0.0005 to 20
- parity_groups: int32 [4, 32], replicated, may hold values from 0 to 7, as said below
Outputs:
- first_quant: bfloat16 [1, 4096, 128, 128], P(None, ('fsdp', 'mp'))
- second_quant: bfloat16 [1, 4096, 128, 128], P(None, ('fsdp', 'mp'))
- first_scale: float32 [1, 4096], P(None, ('fsdp', 'mp'))
- second_scale: float32 [1, 4096], P(None, ('fsdp', 'mp'))
- parity: float32 [128, 2, 1, 32, 128, 128], P(('fsdp', 'mp'))
Inputs may be any that keep to these rules, and one draw needn't show every extreme that they name: `parity_groups`: each row is never falling along fsdp, starts at 0 and names all 8 groups; every group of a row holds 1 to 8 consecutive shards, some group holds exactly 8, and the last group holds only the last shard.
All inputs are finite; a program needn't handle non-finite values. Where the computation divides by a largest or mean magnitude, that divisor is 1e-20 or more.
Results may differ from a plain program's by a relative error of at most 0.005.
Values may be sent and summed in bfloat16 or wider, within the bound.
A program may use at most 128 MiB of HBM per device.

v0:
```python
import jax
import jax.numpy as jnp
from jax import lax
from jax.sharding import PartitionSpec as P

BLK = 128


epsilon = 1e-06


def from_everyone(array, axis):
    devices = lax.axis_size(axis)
    return lax.all_to_all(
        jnp.broadcast_to(array[None], (devices, *array.shape)), axis, 0, 0, tiled=True
    )


def of_everyone(array, axis):
    return from_everyone(array, axis).max(axis=0)


def in_one(arrays, axis):
    ends = [0]
    for a in arrays:
        ends.append(ends[-1] + a.size)
    total = of_everyone(jnp.concatenate([a.ravel() for a in arrays]), axis)
    return tuple((total[b:e].reshape(a.shape) for a, b, e in zip(arrays, ends, ends[1:])))


def side_by_side(arrays, axis, split_dim, concat_dim, along):
    widths = [a.shape[along] for a in arrays]
    both = jnp.concatenate(arrays, axis=along)
    whole = lax.all_to_all(both, axis, split_axis=split_dim, concat_axis=concat_dim, tiled=True)
    return tuple(jnp.split(whole, [sum(widths[:k]) for k in range(1, len(widths))], axis=along))


def shards(first_moment, second_moment, parity_groups):
    layers, row_sets, local_stride, part_rows, columns_all = first_moment.shape
    fsdp_count = lax.axis_size("fsdp")
    model_count = lax.axis_size("mp")
    devices = fsdp_count * model_count
    block_cols = columns_all // BLK
    row_depth = row_sets * block_cols // devices
    row_bands = row_sets // row_depth
    blocks_here = row_depth * local_stride * fsdp_count

    def split_rows(values):
        return values.reshape(
            layers, row_bands, row_depth, local_stride, part_rows, block_cols, BLK
        )

    def arrange(split):
        moved = split.transpose(5, 1, 0, 2, 3, 4, 6)
        return moved.reshape(devices, layers, row_depth, local_stride, part_rows, BLK)

    def assemble(received):
        pieces = received.reshape(
            fsdp_count, model_count, layers, row_depth, local_stride, part_rows, BLK
        )
        return pieces.transpose(2, 3, 0, 4, 1, 5, 6).reshape(layers, blocks_here, BLK, BLK)

    first_split = split_rows(first_moment)
    second_split = split_rows(second_moment)
    first_peak, second_peak = in_one(
        (jnp.max(jnp.abs(first_split), axis=(4, 6)), jnp.max(jnp.abs(second_split), axis=(4, 6))),
        "mp",
    )
    first_local = first_peak + epsilon
    second_local = second_peak + epsilon
    first_arranged = arrange(
        (first_split / first_local[:, :, :, :, None, :, None]).astype(jnp.bfloat16)
    )
    second_arranged = arrange(
        (second_split / second_local[:, :, :, :, None, :, None]).astype(jnp.bfloat16)
    )
    first_sent, second_sent = side_by_side(
        (first_arranged, second_arranged), ("fsdp", "mp"), 0, 0, 1
    )
    first_quant = assemble(first_sent)
    second_quant = assemble(second_sent)

    def scale_order(local):
        return local.transpose(4, 1, 0, 2, 3).reshape(devices, layers, row_depth, local_stride)

    first_came, second_came = side_by_side(
        (scale_order(first_local), scale_order(second_local)), ("fsdp", "mp"), 0, 0, 1
    )

    def scale_list(came):
        picked = came.reshape(fsdp_count, model_count, layers, row_depth, local_stride)[:, 0]
        return picked.transpose(1, 2, 0, 3).reshape(layers, blocks_here)

    first_scale = scale_list(first_came)
    second_scale = scale_list(second_came)
    index = jnp.arange(devices, dtype=jnp.int32)
    fsdp_of = index // model_count
    model_of = index % model_count
    group_of = parity_groups[model_of, fsdp_of]
    before_group = parity_groups[model_of, (fsdp_of + fsdp_count - 1) % fsdp_count]
    leading = (fsdp_of == 0) | (group_of != before_group)
    member = (
        leading[:, None]
        & (model_of[:, None] == model_of[None, :])
        & (group_of[None, :] == before_group[:, None])
    )
    weights = member.astype(jnp.float32)
    both = jnp.stack(
        [first_arranged.astype(jnp.float32), second_arranged.astype(jnp.float32)], axis=1
    )
    flat = both.reshape(devices, -1)
    sums = jnp.dot(weights, flat, precision=lax.Precision.HIGHEST)
    received = lax.all_to_all(sums, ("fsdp", "mp"), split_axis=0, concat_axis=0, tiled=True)
    unpacked = received.reshape(devices, 2, layers, row_depth, local_stride, part_rows, BLK)
    parity = jnp.stack([assemble(unpacked[:, 0]), assemble(unpacked[:, 1])])[None]
    return (first_quant, second_quant, first_scale, second_scale, parity)


def solution(mesh):
    in_specs = (P(None, None, "fsdp", "mp", None), P(None, None, "fsdp", "mp", None), P())
    out_specs = (
        P(None, ("fsdp", "mp"), None, None),
        P(None, ("fsdp", "mp"), None, None),
        P(None, ("fsdp", "mp")),
        P(None, ("fsdp", "mp")),
        P(("fsdp", "mp"), None, None, None, None, None),
    )
    return jax.shard_map(shards, mesh=mesh, in_specs=in_specs, out_specs=out_specs, check_vma=False)
```

profile of v0, /device:TPU:1, one launch (start us, length us, event | category | flops | bytes accessed | tf_op | source)
XLA Modules:
  0.0 131.3 jit_solution(11447676772605685803)
XLA Ops:
  0.7 2.0 %abs_reduce_fusion.1 = f32[16,1024]{1,0:T(8,128)S(1)} fusion(f32[1,16,1,32,1024]{4,3,2,1,0:T(8,128)} %param.3), kind=kLoop, calls=%fused_computation.9 | loop fusion | flops 1032192 | bytes 2162688 | tf_op jit(solution)/shard_map/reduce_max | solution.py:66
  4.1 5.8 %all-to-all-start = ((f32[4,1,256]{2,1,0:T(1,128)}), f32[4,1,256]{2,1,0:T(1,128)S(1)}, u32[]{:S(2)}, u32[]{:S(2)}) async-start(f32[4,1,256]{2,1,0:T(1,128)} %broadcast_in_dim.4), calls=%async_computation | async-start | bytes 8192 | tf_op jit(solution)/shard_map/all_to_all | solution.py:14
  9.8 1.8 %copy.75 = f32[64,8,8,128]{3,2,1,0:T(8,128)} copy(f32[64,8,8,128]{3,1,2,0:T(8,128)S(1)} %bitcast.55) | data formatting | bytes 4194304
  12.3 2.2 %all-to-all-done = f32[4,1,256]{2,1,0:T(1,128)S(1)} async-done(((f32[4,1,256]{2,1,0:T(1,128)}), f32[4,1,256]{2,1,0:T(1,128)S(1)}, u32[]{:S(2)}, u32[]{:S(2)}) %all-to-all-start) | async-done | bytes 4128 | tf_op jit(solution)/shard_map/all_to_all | solution.py:14
  15.2 0.7 copy.64
  15.9 8.4 %all-to-all-start.2 = ((f32[128,2,1,1]{1,3,2,0:T(1,128)}), f32[128,2,1,1]{1,3,2,0:T(1,128)S(1)}, u32[]{:S(2)}, u32[]{:S(2)}) async-start(f32[128,2,1,1]{1,3,2,0:T(1,128)} %copy.64), calls=%async_computation.2 | async-start | bytes 131072 | tf_op jit(solution)/shard_map/all_to_all | solution.py:34
  24.3 1.9 %fusion.1 = bf16[8,16,1,1,1,32,128]{6,0,3,5,1,4,2:T(8,128)(2,1)S(1)} fusion(f32[1,16,1,1,32,8,128]{6,5,2,4,1,3,0:T(8,128)} %bitcast.58, f32[16,8]{1,0:T(8,128)S(1)} %add.140), kind=kLoop, calls=%fused_computation.11 | loop fusion | flops 1048576 | bytes 3146240 | tf_op jit(solution)/shard_map/transpose | solution.py:54
  27.1 2.1 %copy.61 = bf16[128,2,1,1,32,128]{5,4,3,2,1,0:T(8,128)(2,1)} copy(bf16[128,2,1,1,32,128]{5,4,0,3,2,1:T(8,128)(2,1)S(1)} %pad_maximum_fusion) | data formatting | bytes 4194304 | tf_op jit(solution)/shard_map/concatenate | solution.py:33
  29.1 4.5 %all-to-all-done.2 = f32[128,2,1,1]{1,3,2,0:T(1,128)S(1)} async-done(((f32[128,2,1,1]{1,3,2,0:T(1,128)}), f32[128,2,1,1]{1,3,2,0:T(1,128)S(1)}, u32[]{:S(2)}, u32[]{:S(2)}) %all-to-all-start.2) | async-done | bytes 1056 | tf_op jit(solution)/shard_map/all_to_all | solution.py:34
  33.6 5.7 %all-to-all-start.1 = ((bf16[128,2,1,1,32,128]{5,4,3,2,1,0:T(8,128)(2,1)}), bf16[128,2,1,1,32,128]{5,4,3,2,1,0:T(8,128)(2,1)}, u32[]{:S(2)}, u32[]{:S(2)}) async-start(bf16[128,2,1,1,32,128]{5,4,3,2,1,0:T(8,128)(2,1)} %copy.61), calls=%async_computation.1 | async-start | bytes 4194304 | tf_op jit(solution)/shard_map/all_to_all | solution.py:34
  39.4 1.5 %gather_fusion = s32[128]{0:T(128)S(1)} fusion(s32[4,32]{1,0:T(4,128)S(1)} %copy-done, s32[128]{0:T(128)S(1)} %fusion.21), kind=kCustom, calls=%fused_computation | custom fusion | bytes 2048 | tf_op jit(solution)/shard_map/gather | solution.py:99
  41.0 1.5 %gather_fusion.1 = s32[128]{0:T(128)S(1)} fusion(s32[4,32]{1,0:T(4,128)S(1)} %copy-done, s32[128]{0:T(128)S(1)} %fusion.20), kind=kCustom, calls=%fused_computation.1 | custom fusion | bytes 2048 | tf_op jit(solution)/shard_map/gather | solution.py:100
  42.5 1.5 %pad_maximum_fusion.1 = bf16[128,2,1,1,1,32,128]{6,5,0,4,3,2,1:T(8,128)(2,1)} fusion(bf16[128,1,1,1,1,32,128]{6,5,0,4,3,2,1:T(8,128)(2,1)S(1)} %bitcast.52, bf16[128,1,1,1,1,32,128]{6,5,0,4,3,2,1:T(8,128)(2,1)S(1)} %bitcast.54), kind=kLoop, calls=%fused_computation.5 | loop fusion | flops 1048576 | bytes 4194304 | tf_op jit(solution)/shard_map/stack | solution.py:108
  44.0 3.5 %copy.67 = bf16[128,2,1,1,1,32,128]{0,6,5,1,4,3,2:T(8,128)(2,1)S(1)} copy(bf16[128,2,1,1,1,32,128]{6,5,0,4,3,2,1:T(8,128)(2,1)} %pad_maximum_fusion.1) | data formatting | bytes 4194304 | tf_op jit(solution)/shard_map/stack | solution.py:108
  47.5 0.8 convolution_bitcast_fusion
  48.3 6.4 %copy.68 = f32[128,1,8192]{2,1,0:T(1,128)} copy(f32[128,1,8192]{2,0,1:T(8,128)S(1)} %convolution_bitcast_fusion) | data formatting | bytes 8388608 | tf_op jit(solution)/shard_map/all_to_all | solution.py:113
  54.6 14.5 %all-to-all-done.1 = bf16[128,2,1,1,32,128]{5,4,3,2,1,0:T(8,128)(2,1)} async-done(((bf16[128,2,1,1,32,128]{5,4,3,2,1,0:T(8,128)(2,1)}), bf16[128,2,1,1,32,128]{5,4,3,2,1,0:T(8,128)(2,1)}, u32[]{:S(2)}, u32[]{:S(2)}) %all-to-all-start.1) | async-done | bytes 2097184 | tf_op jit(solution)/shard_map/all_to_all | solution.py:34
  69.1 5.2 %all-to-all-start.3 = ((f32[128,1,8192]{2,1,0:T(1,128)}), f32[128,1,8192]{2,1,0:T(1,128)}, u32[]{:S(2)}, u32[]{:S(2)}) async-start(f32[128,1,8192]{2,1,0:T(1,128)} %copy.68), calls=%async_computation.3 | async-start | bytes 8388608 | tf_op jit(solution)/shard_map/all_to_all | solution.py:113
  74.4 2.2 %slice_reduce_fusion = (f32[128]{0:T(128)S(1)}, f32[128]{0:T(128)S(1)}) fusion(f32[128,2,1,1]{1,3,2,0:T(1,128)S(1)} %all-to-all-done.2), kind=kLoop, calls=%fused_computation.12 | loop fusion | bytes 2048 | tf_op jit(solution)/shard_map/split | solution.py:35
  76.7 0.6 slice_reduce_fusion.2
  78.0 3.2 %fusion.23 = (bf16[128,1,1,1,32,128]{5,4,3,2,1,0:T(8,128)(2,1)}, bf16[128,1,1,1,32,128]{5,4,3,2,1,0:T(8,128)(2,1)}) fusion(bf16[128,2,1,1,32,128]{5,4,3,2,1,0:T(8,128)(2,1)} %all-to-all-done.1), kind=kLoop, calls=%fused_computation.58 | loop fusion | bytes 4194304 | tf_op jit(solution)/shard_map/split | solution.py:35
  81.2 45.1 %all-to-all-done.3 = f32[128,1,8192]{2,1,0:T(1,128)} async-done(((f32[128,1,8192]{2,1,0:T(1,128)}), f32[128,1,8192]{2,1,0:T(1,128)}, u32[]{:S(2)}, u32[]{:S(2)}) %all-to-all-start.3) | async-done | bytes 4194336 | tf_op jit(solution)/shard_map/all_to_all | solution.py:113
  126.4 2.7 %fusion.22 = (f32[128,1,1,1,1,32,128]{6,5,1,0,4,3,2:T(8,128)S(1)}, f32[128,1,1,1,1,32,128]{6,5,1,0,4,3,2:T(8,128)S(1)}) fusion(f32[128,2,1,1,1,32,128]{6,5,1,0,4,3,2:T(8,128)} %bitcast.14), kind=kLoop, calls=%fused_computation.57 | loop fusion | bytes 8388608 | tf_op jit(solution)/shard_map/slice | solution.py:115
  129.0 2.3 %maximum_bitcast_fusion = f32[1,2,1,32,128,128]{5,4,3,2,1,0:T(8,128)} fusion(f32[1,1,32,128,128]{4,3,2,0,1:T(8,128)S(1)} %bitcast.61, f32[1,1,32,128,128]{4,3,2,0,1:T(8,128)S(1)} %bitcast.60), kind=kLoop, calls=%fused_computation.3 | loop fusion | flops 1048576 | bytes 8388608 | tf_op jit(solution)/shard_map/broadcast_in_dim | solution.py:115
  (38 shorter events, 4.4 us)
Async XLA Ops:
  0.6 38.8 %copy-start = (s32[4,32]{1,0:T(4,128)S(1)}, s32[4,32]{1,0:T(4,128)}, u32[]{:S(2)}) copy-start(s32[4,32]{1,0:T(4,128)} %param.5) | copy-start | bytes 1540
  0.6 2.3 %copy-start.1 = (f32[1,16,1,32,1024]{4,3,2,1,0:T(8,128)S(1)}, f32[1,16,1,32,1024]{4,3,2,1,0:T(8,128)}, u32[]{:S(2)}) copy-start(f32[1,16,1,32,1024]{4,3,2,1,0:T(8,128)} %param.4) | copy-start | bytes 6291460
  4.1 10.4 %all-to-all-start = ((f32[4,1,256]{2,1,0:T(1,128)}), f32[4,1,256]{2,1,0:T(1,128)S(1)}, u32[]{:S(2)}, u32[]{:S(2)}) async-start(f32[4,1,256]{2,1,0:T(1,128)} %broadcast_in_dim.4), calls=%async_computation | async-start | bytes 8192 | tf_op jit(solution)/shard_map/all_to_all | solution.py:14
  9.8 2.0 %copy-start.2 = (f32[1,16,1,32,1024]{4,3,2,1,0:T(8,128)S(1)}, f32[1,16,1,32,1024]{4,3,2,1,0:T(8,128)}, u32[]{:S(2)}) copy-start(f32[1,16,1,32,1024]{4,3,2,1,0:T(8,128)} %param.3) | copy-start | bytes 6291460
  15.9 17.7 %all-to-all-start.2 = ((f32[128,2,1,1]{1,3,2,0:T(1,128)}), f32[128,2,1,1]{1,3,2,0:T(1,128)S(1)}, u32[]{:S(2)}, u32[]{:S(2)}) async-start(f32[128,2,1,1]{1,3,2,0:T(1,128)} %copy.64), calls=%async_computation.2 | async-start | bytes 131072 | tf_op jit(solution)/shard_map/all_to_all | solution.py:34
  33.6 35.5 %all-to-all-start.1 = ((bf16[128,2,1,1,32,128]{5,4,3,2,1,0:T(8,128)(2,1)}), bf16[128,2,1,1,32,128]{5,4,3,2,1,0:T(8,128)(2,1)}, u32[]{:S(2)}, u32[]{:S(2)}) async-start(bf16[128,2,1,1,32,128]{5,4,3,2,1,0:T(8,128)(2,1)} %copy.61), calls=%async_computation.1 | async-start | bytes 4194304 | tf_op jit(solution)/shard_map/all_to_all | solution.py:34
  69.1 57.2 %all-to-all-start.3 = ((f32[128,1,8192]{2,1,0:T(1,128)}), f32[128,1,8192]{2,1,0:T(1,128)}, u32[]{:S(2)}, u32[]{:S(2)}) async-start(f32[128,1,8192]{2,1,0:T(1,128)} %copy.68), calls=%async_computation.3 | async-start | bytes 8388608 | tf_op jit(solution)/shard_map/all_to_all | solution.py:113
where the time goes:
time: 132 us; the launch traced here: 131 us
  waiting for transfers between devices  66.2 us (50%)
  local copies, waits for them, and re-layouts  29.5 us (22%)
  starting transfers between devices  25.1 us (19%)
  other arithmetic  8.82 us (7%)
    all_to_all x1, waiting for transfers between devices, shards(): lax.all_to_all(sums, ('fsdp', 'mp'), split_axis=0, concat_axis=0, tiled=T...  45.1 us
    all_to_all x2, waiting for transfers between devices, side_by_side(): lax.all_to_all(both, axis, split_axis=split_dim, concat_axis=concat_dim,...  19 us
    all_to_all x2, starting transfers between devices, side_by_side(): lax.all_to_all(both, axis, split_axis=split_dim, concat_axis=concat_dim,...  14.1 us
    all_to_all x1, local copies, waits for them, and re-layouts, shards(): lax.all_to_all(sums, ('fsdp', 'mp'), split_axis=0, concat_axis=0, tiled=T...  6.37 us
    all_to_all x1, starting transfers between devices, from_everyone(): lax.all_to_all(jnp.broadcast_to(array[None], (devices, *array.shape)), ax...  5.78 us
    split x2, local copies, waits for them, and re-layouts, side_by_side(): jnp.split(whole, [sum(widths[:k]) for k in range(1, len(widths))], axis=a...  5.4 us
    all_to_all x1, starting transfers between devices, shards(): lax.all_to_all(sums, ('fsdp', 'mp'), split_axis=0, concat_axis=0, tiled=T...  5.21 us
    another operation x1, local copies, waits for them, and re-layouts, shards(): jnp.stack([first_arranged.astype(jnp.float32), second_arranged.astype(jnp...  3.49 us
  transfers between devices with their start and end apart: 4, of which 4 were waited for; matrix products, arithmetic and copies ran while one was open for 22% of the time, Pallas kernels for 0%

commit v1 on v0

v1 whole, which is shorter than its diff:
```python
import functools

import jax
import jax.numpy as jnp
from jax import lax
from jax.experimental import pallas as pl
from jax.experimental.pallas import tpu as pltpu
from jax.sharding import PartitionSpec as P

MESH = pl.DeviceIdType.MESH
BLK = 128
FS = 32
MP = 4
N = FS * MP
ROWS = BLK // MP
COLS = 8
SETS = 16
CHUNKS = 4
epsilon = 1e-06

QUAD = ((0, 0), (0, 1), (2, 0), (2, 1))


def where_am_i():
    f = lax.axis_index("fsdp")
    m = lax.axis_index("mp")
    return f, m


def target(f, m, step, dx2, dc):
    dy = step % 4
    dx = (step // 4) % 2 + dx2
    dz = step // 8
    z = (f // 8 + dz) % 4
    x = ((m // 2) * 2 + (f // 4) % 2 + dx) % 4
    y = (f % 4 + dy) % 4
    return z * 8 + (x % 2) * 4 + y, (x // 2) * 2 + (m % 2 + dc) % 2


def source_row(f, m, step):
    dy = step % 4
    dx = (step // 4) % 2
    dz = step // 8
    z = (f // 8 + 4 - dz) % 4
    xl = ((f // 4) % 2 + 2 - dx) % 2
    y = (f % 4 + 4 - dy) % 4
    return z * 8 + xl * 4 + y


def order(j):
    return (13 * j) % 32


def kernel(
    groups, first, second,
    first_quant, second_quant, first_scale, second_scale, parity,
    x, send_q, send_p, recv_q, recv_p,
    partial, peak_send, peak_recv, scale_send, scale_recv,
    in_sem, qs_sem, qr_sem, ps_sem, pr_sem, ks_sem, kr_sem, ss_sem, sr_sem,
):
    f, m = where_am_i()
    me = f * MP + m

    barrier = pltpu.get_barrier_semaphore()

    loads = []
    for t, ref in enumerate((first, second)):
        for b in range(CHUNKS):
            w = SETS // CHUNKS
            load = pltpu.make_async_copy(
                ref.at[pl.ds(b * w, w)], x.at[t, pl.ds(b * w, w)], in_sem.at[t * CHUNKS + b]
            )
            load.start()
            loads.append(load)

    def greet(d, carry):
        other = (me + d) % N
        pl.semaphore_signal(
            barrier, inc=1, device_id=(other // MP, other % MP), device_id_type=MESH
        )
        return carry

    lax.fori_loop(1, N, greet, 0)

    for t in range(2):
        for b in range(CHUNKS):
            loads[t * CHUNKS + b].wait()
            w = SETS // CHUNKS

            def cast(q, carry):
                for c in range(COLS):
                    v = x[t, q, :, c * BLK : (c + 1) * BLK]
                    send_q[c * SETS + q, t] = v.astype(jnp.bfloat16)
                    a = jnp.abs(v)
                    a = jnp.maximum(
                        jnp.maximum(a[0:8], a[8:16]), jnp.maximum(a[16:24], a[24:32])
                    )
                    partial[t, c * SETS + q] = a
                return carry

            lax.fori_loop(b * w, (b + 1) * w, cast, 0)
        rows = jnp.max(partial[t], axis=1)
        peak_send[t : t + 1, :] = jnp.max(rows.T, axis=0, keepdims=True)

    pl.semaphore_wait(barrier, N - 1)

    for k in range(1, MP):
        pltpu.make_async_remote_copy(
            src_ref=peak_send, dst_ref=peak_recv.at[m], send_sem=ks_sem, recv_sem=kr_sem,
            device_id=(f, (m + k) % MP), device_id_type=MESH,
        ).start()

    def send(src, dst, s_sem, r_sem, step, dx2, dc):
        tf, tm = target(f, m, step, dx2, dc)
        pltpu.make_async_remote_copy(
            src_ref=src.at[tf * MP + tm], dst_ref=dst.at[f, m], send_sem=s_sem,
            recv_sem=r_sem.at[f], device_id=(tf, tm), device_id_type=MESH,
        ).start()

    def send_all(src, dst, s_sem, r_sem):
        def one(j, carry):
            for dx2, dc in QUAD:
                send(src, dst, s_sem, r_sem, order(j), dx2, dc)
            return carry

        lax.fori_loop(1, FS, one, 0)
        for dx2, dc in QUAD[1:]:
            send(src, dst, s_sem, r_sem, 0, dx2, dc)

    send_all(send_q, recv_q, qs_sem, qr_sem)
    recv_q[f, m] = send_q[me]

    peak_recv[m] = peak_send[...]
    pltpu.make_async_copy(
        peak_recv.at[pl.ds(0, MP - 1)], peak_recv.at[pl.ds(0, MP - 1)], kr_sem
    ).wait()
    scale = jnp.max(peak_recv[...], axis=0) + epsilon
    for t in range(2):
        wide = jnp.broadcast_to(scale[t : t + 1], (BLK, N)).T
        scale_send[:, t, :] = wide

    def send_scale(j, carry):
        tf = (f + order(j)) % FS
        pltpu.make_async_remote_copy(
            src_ref=scale_send.at[tf * MP + m], dst_ref=scale_recv.at[f], send_sem=ss_sem,
            recv_sem=sr_sem, device_id=(tf, m), device_id_type=MESH,
        ).start()
        return carry

    lax.fori_loop(1, FS, send_scale, 0)
    scale_recv[f] = scale_send[me]

    for row in range(MP):

        def add(i, sums):
            d = i * MP + row
            before = groups[row, jnp.maximum(i - 1, 0)]
            lead = (groups[row, i] != before).astype(jnp.float32)
            keep = 1.0 - lead
            c = d // SETS
            q = d % SETS
            out = []
            for t in range(2):
                inv = 1.0 / scale_send[d, pl.ds(t, 1), :]
                v = x[t, q, :, pl.ds(pl.multiple_of(c * BLK, BLK), BLK)]
                v = (v * inv).astype(jnp.bfloat16).astype(jnp.float32)
                send_p[d, t] = (sums[t] * lead).astype(jnp.bfloat16)
                out.append(sums[t] * keep + v)
            return tuple(out)

        zero = jnp.zeros((ROWS, BLK), jnp.float32)
        last = lax.fori_loop(0, FS, add, (zero, zero))
        for t in range(2):
            send_p[row, t] = last[t].astype(jnp.bfloat16)

    send_all(send_p, recv_p, ps_sem, pr_sem)
    recv_p[f, m] = send_p[me]

    pltpu.make_async_copy(
        scale_recv.at[pl.ds(0, FS - 1)], scale_recv.at[pl.ds(0, FS - 1)], sr_sem
    ).wait()
    eye = lax.broadcasted_iota(jnp.int32, (FS, BLK), 0) == lax.broadcasted_iota(
        jnp.int32, (FS, BLK), 1
    )
    for t, ref in enumerate((first_scale, second_scale)):
        came = scale_recv[:, t, :]
        ref[...] = jnp.sum(jnp.where(eye, came, 0.0), axis=0, keepdims=True)[:, :FS]

    quants = (first_quant, second_quant)

    def finish_q(k):
        for t in range(2):
            inv = 1.0 / scale_recv[k, pl.ds(t, 1), :]
            for r in range(MP):
                v = recv_q[k, r, t].astype(jnp.float32)
                quants[t][k, r * ROWS : (r + 1) * ROWS, :] = (v * inv).astype(jnp.bfloat16)

    def finish_p(k):
        for t in range(2):
            for r in range(MP):
                parity[t, k, r * ROWS : (r + 1) * ROWS, :] = recv_p[k, r, t].astype(jnp.float32)

    def take(buf, sem, finish):
        def one(j, carry):
            k = source_row(f, m, order(j))
            pltpu.make_async_copy(buf.at[k], buf.at[k], sem.at[k]).wait()
            finish(k)
            return carry

        lax.fori_loop(1, FS, one, 0)
        pltpu.make_async_copy(
            buf.at[f, pl.ds(0, MP - 1)], buf.at[f, pl.ds(0, MP - 1)], sem.at[f]
        ).wait()
        finish(f)

    take(recv_q, qr_sem, finish_q)
    take(recv_p, pr_sem, finish_p)

    for src, sem in ((send_q, qs_sem), (send_p, ps_sem)):
        part = src.at[pl.ds(0, N - 1)]
        pltpu.make_async_copy(part, part, sem).wait()
    part = scale_send.at[pl.ds(0, FS - 1)]
    pltpu.make_async_copy(part, part, ss_sem).wait()
    part = peak_recv.at[pl.ds(0, MP - 1)]
    pltpu.make_async_copy(part, part, ks_sem).wait()


def shards(first_moment, second_moment, parity_groups):
    hbm = pl.BlockSpec(memory_space=pltpu.HBM)
    vmem = pl.BlockSpec(memory_space=pltpu.VMEM)
    dma = pltpu.SemaphoreType.DMA
    f32, bf16 = jnp.float32, jnp.bfloat16
    fq, sq, fs, ss, par = pl.pallas_call(
        kernel,
        out_shape=(
            jax.ShapeDtypeStruct((FS, BLK, BLK), bf16),
            jax.ShapeDtypeStruct((FS, BLK, BLK), bf16),
            jax.ShapeDtypeStruct((1, FS), f32),
            jax.ShapeDtypeStruct((1, FS), f32),
            jax.ShapeDtypeStruct((2, FS, BLK, BLK), f32),
        ),
        in_specs=[pl.BlockSpec(memory_space=pltpu.SMEM), hbm, hbm],
        out_specs=(vmem, vmem, vmem, vmem, vmem),
        scratch_shapes=[
            pltpu.VMEM((2, SETS, ROWS, COLS * BLK), f32),
            pltpu.VMEM((N, 2, ROWS, BLK), bf16),
            pltpu.VMEM((N, 2, ROWS, BLK), bf16),
            pltpu.VMEM((FS, MP, 2, ROWS, BLK), bf16),
            pltpu.VMEM((FS, MP, 2, ROWS, BLK), bf16),
            pltpu.VMEM((2, N, 8, BLK), f32),
            pltpu.VMEM((2, N), f32),
            pltpu.VMEM((MP, 2, N), f32),
            pltpu.VMEM((N, 2, BLK), f32),
            pltpu.VMEM((FS, 2, BLK), f32),
            dma((2 * CHUNKS,)),
            dma, dma((FS,)),
            dma, dma((FS,)),
            dma, dma,
            dma, dma,
        ],
        compiler_params=pltpu.CompilerParams(
            collective_id=0, has_side_effects=True, vmem_limit_bytes=40 << 20
        ),
        name="relayout",
    )(
        parity_groups,
        first_moment.reshape(SETS, ROWS, COLS * BLK),
        second_moment.reshape(SETS, ROWS, COLS * BLK),
    )
    return fq[None], sq[None], fs, ss, par.reshape(1, 2, 1, FS, BLK, BLK)


def solution(mesh):
    in_specs = (P(None, None, "fsdp", "mp", None), P(None, None, "fsdp", "mp", None), P())
    out_specs = (
        P(None, ("fsdp", "mp"), None, None),
        P(None, ("fsdp", "mp"), None, None),
        P(None, ("fsdp", "mp")),
        P(None, ("fsdp", "mp")),
        P(("fsdp", "mp"), None, None, None, None, None),
    )
    return jax.shard_map(shards, mesh=mesh, in_specs=in_specs, out_specs=out_specs, check_vma=False)
```

time: 132 us -> 72.7 us (0.55)
  waiting for transfers between devices: 66.2 us -> 0 us
  Pallas kernels: 0 us -> 63 us
  starting transfers between devices: 25.1 us -> 0 us
  local copies, waits for them, and re-layouts: 29.5 us -> 8.83 us
  other arithmetic: 8.82 us -> 0 us
    all_to_all x4 -> x0, waiting for transfers between devices: 66.2 us -> none  [the longest x1 45.1 us: shards(): lax.all_to_all(sums, ('fsdp', 'mp'), split_axis=0, concat_axis=0, tiled=T...]
    pallas_call x0 -> x1, Pallas kernels: none -> 63 us  [shards(): pl.pallas_call(kernel, out_shape=(jax.ShapeDtypeStruct((FS, BLK, BLK), bf...]
    all_to_all x4 -> x0, starting transfers between devices: 25.1 us -> none  [the longest x2 14.1 us: side_by_side(): lax.all_to_all(both, axis, split_axis=split_dim, concat_axis=concat_dim,...]
    all_to_all x1 -> x0, local copies, waits for them, and re-layouts: 6.37 us -> none  [shards(): lax.all_to_all(sums, ('fsdp', 'mp'), split_axis=0, concat_axis=0, tiled=T...]
    unnamed x10 -> x11, local copies, waits for them, and re-layouts: 2.48 us -> 8.83 us
    split x2 -> x0, local copies, waits for them, and re-layouts: 5.4 us -> none  [side_by_side(): jnp.split(whole, [sum(widths[:k]) for k in range(1, len(widths))], axis=a...]
    slice x3 -> x0, local copies, waits for them, and re-layouts: 3.94 us -> none  [the longest x1 2.69 us: shards(): unpacked[:, 0]]
    another operation x1 -> x0, local copies, waits for them, and re-layouts: 3.49 us -> none  [shards(): jnp.stack([first_arranged.astype(jnp.float32), second_arranged.astype(jnp...]
  transfers between devices with their start and end apart: 4 -> 0, of which waited for: 4 -> 0; matrix products, arithmetic and copies ran while one was open for 22% -> 0% of each run, Pallas kernels for 0% -> 0%
where the time goes in v1:
time: 72.7 us; the launch traced here: 72.5 us
  Pallas kernels  63 us (87%)
  local copies, waits for them, and re-layouts  8.83 us (12%)
    pallas_call x1, Pallas kernels, shards(): pl.pallas_call(kernel, out_shape=(jax.ShapeDtypeStruct((FS, BLK, BLK), bf...  63 us
    unnamed x11, local copies, waits for them, and re-layouts  8.83 us

profile of v1, /device:TPU:1, one launch (start us, length us, event | category | flops | bytes accessed | tf_op | source)
XLA Modules:
  0.0 72.5 jit_solution(7216982700309224958)
XLA Ops:
  0.6 0.0 copy-start
  0.6 1.6 %copy-done = f32[1,16,1,32,1024]{4,3,2,1,0:T(8,128)S(1)} copy-done((f32[1,16,1,32,1024]{4,3,2,1,0:T(8,128)S(1)}, f32[1,16,1,32,1024]{4,3,2,1,0:T(8,128)}, u32[]{:S(2)}) %copy-start) | copy-done | bytes 2097176
  2.2 0.0 copy-start.1
  2.2 1.6 %copy-done.1 = f32[1,16,1,32,1024]{4,3,2,1,0:T(8,128)S(1)} copy-done((f32[1,16,1,32,1024]{4,3,2,1,0:T(8,128)S(1)}, f32[1,16,1,32,1024]{4,3,2,1,0:T(8,128)}, u32[]{:S(2)}) %copy-start.1) | copy-done | bytes 2097176
  3.8 0.0 copy-start.2
  3.8 0.7 copy-done.2
  4.5 63.0 %relayout.1 = (bf16[32,128,128]{2,1,0:T(8,128)(2,1)S(1)}, bf16[32,128,128]{2,1,0:T(8,128)(2,1)S(1)}, f32[1,32]{1,0:T(1,128)S(1)}, f32[1,32]{1,0:T(1,128)S(1)}, f32[2,32,128,128]{3,2,1,0:T(8,128)S(1)}) custom-call(s32[4,32]{1,0:T(4,128)S(1)} %copy-done.2, f32[16,32,1024]{2,1,0:T(8,128)S(1)} %bitcast.8, f32[16,32,1024]{2,1,0:T(8,128)S(1)} %bitcast.9), custom_call_target="tpu_custom_call" | custom-call | tf_op jit(solution)/shard_map/relayout/pallas_call | solution.py:233
  67.5 1.0 %copy.14 = bf16[1,32,128,128]{3,2,1,0:T(8,128)(2,1)} copy(bf16[1,32,128,128]{3,2,1,0:T(8,128)(2,1)S(1)} %bitcast.11) | data formatting | bytes 2097152
  68.5 1.0 %copy.15 = bf16[1,32,128,128]{3,2,1,0:T(8,128)(2,1)} copy(bf16[1,32,128,128]{3,2,1,0:T(8,128)(2,1)S(1)} %bitcast.10) | data formatting | bytes 2097152
  69.4 0.5 copy.16
  69.9 0.5 copy.17
  70.5 2.0 %copy.18 = f32[1,2,1,32,128,128]{5,4,3,2,1,0:T(8,128)} copy(f32[1,2,1,32,128,128]{5,4,3,2,1,0:T(8,128)S(1)} %bitcast.7) | data formatting | bytes 8388608
Async XLA Ops:
  0.6 1.6 %copy-start = (f32[1,16,1,32,1024]{4,3,2,1,0:T(8,128)S(1)}, f32[1,16,1,32,1024]{4,3,2,1,0:T(8,128)}, u32[]{:S(2)}) copy-start(f32[1,16,1,32,1024]{4,3,2,1,0:T(8,128)} %param.3) | copy-start | bytes 6291460
  2.2 1.6 %copy-start.1 = (f32[1,16,1,32,1024]{4,3,2,1,0:T(8,128)S(1)}, f32[1,16,1,32,1024]{4,3,2,1,0:T(8,128)}, u32[]{:S(2)}) copy-start(f32[1,16,1,32,1024]{4,3,2,1,0:T(8,128)} %param.4) | copy-start | bytes 6291460
  3.8 0.7 copy-start.2

commit v2 on v1

v2 whole, which is shorter than its diff:
```python
import jax
import jax.numpy as jnp
from jax import lax
from jax.experimental import pallas as pl
from jax.experimental.pallas import tpu as pltpu
from jax.sharding import PartitionSpec as P

LOGICAL = pl.DeviceIdType.LOGICAL
BLK = 128
FS = 32
MP = 4
N = FS * MP
ROWS = BLK // MP
COLS = 8
SETS = 16
CHUNKS = 4
PARTS = 8
epsilon = 1e-06

def distance(step):
    return sum(min(v, 4 - v) for v in step[:3])


STEPS = [
    (i // 32, (i // 8) % 4, (i // 2) % 4, i % 2) for i in ((n * 53) % N for n in range(1, N))
]
STEPS.sort(key=lambda step: -distance(step))


def target(f, m, step):
    dz, dx, dy, dc = step
    z = (f // 8 + dz) % 4
    x = ((m // 2) * 2 + (f // 4) % 2 + dx) % 4
    y = (f % 4 + dy) % 4
    return (z * 8 + (x % 2) * 4 + y) * MP + (x // 2) * 2 + (m % 2 + dc) % 2


def wait_all(ref, sem, count):
    part = ref.at[pl.ds(0, count)]
    pltpu.make_async_copy(part, part, sem).wait()


def kernel(
    groups_in, first, second,
    first_quant, second_quant, scales, recv_p,
    groups, x, send_q, send_p, recv_q,
    partial, peak_send, peak_recv, scale_send, scale_recv,
    in_sem, g_sem, qs_sem, qr_sem, ps_sem, pr_sem, ks_sem, kr_sem, ss_sem, sr_sem,
):
    f = lax.axis_index("fsdp")
    m = lax.axis_index("mp")
    me = f * MP + m

    barrier = pltpu.get_barrier_semaphore()

    groups_load = pltpu.make_async_copy(groups_in, groups, g_sem)
    groups_load.start()
    loads = []
    for t, ref in enumerate((first, second)):
        for b in range(CHUNKS):
            w = SETS // CHUNKS
            load = pltpu.make_async_copy(
                ref.at[pl.ds(b * w, w)], x.at[t, pl.ds(b * w, w)], in_sem.at[t * CHUNKS + b]
            )
            load.start()
            loads.append(load)

    others = [target(f, m, step) for step in STEPS]
    for other in others:
        pl.semaphore_signal(barrier, inc=1, device_id=other, device_id_type=LOGICAL)

    for t in range(2):
        for b in range(CHUNKS):
            loads[t * CHUNKS + b].wait()
            w = SETS // CHUNKS

            def cast(q, carry):
                for c in range(COLS):
                    v = x[t, q, :, c * BLK : (c + 1) * BLK]
                    send_q[c * SETS + q, t] = v.astype(jnp.bfloat16)
                    a = jnp.abs(v)
                    a = jnp.maximum(
                        jnp.maximum(a[0:8], a[8:16]), jnp.maximum(a[16:24], a[24:32])
                    )
                    partial[t, c * SETS + q] = a
                return carry

            lax.fori_loop(b * w, (b + 1) * w, cast, 0)
        rows = jnp.max(partial[t], axis=1)
        peak_send[t : t + 1, :] = jnp.max(rows.T, axis=0, keepdims=True)

    pl.semaphore_wait(barrier, N - 1)

    for k in range(1, MP):
        pltpu.make_async_remote_copy(
            src_ref=peak_send, dst_ref=peak_recv.at[m], send_sem=ks_sem, recv_sem=kr_sem,
            device_id=f * MP + (m + k) % MP, device_id_type=LOGICAL,
        ).start()

    def send_all(src, dst, s_sem, r_sem):
        for other in others:
            pltpu.make_async_remote_copy(
                src_ref=src.at[other], dst_ref=dst.at[f, m], send_sem=s_sem, recv_sem=r_sem,
                device_id=other, device_id_type=LOGICAL,
            ).start()

    send_all(send_q, recv_q, qs_sem, qr_sem)
    recv_q[f, m] = send_q[me]

    peak_recv[m] = peak_send[...]
    wait_all(peak_recv, kr_sem, MP - 1)
    scale = jnp.max(peak_recv[...], axis=0) + epsilon
    for t in range(2):
        wide = jnp.broadcast_to(scale[t : t + 1], (BLK, N)).T
        scale_send[:, t, :] = wide

    def send_scale(j, carry):
        other = (me + j * MP) % N
        pltpu.make_async_remote_copy(
            src_ref=scale_send.at[other], dst_ref=scale_recv.at[f], send_sem=ss_sem,
            recv_sem=sr_sem, device_id=other, device_id_type=LOGICAL,
        ).start()
        return carry

    lax.fori_loop(1, FS, send_scale, 0)
    scale_recv[f] = scale_send[me]

    groups_load.wait()

    for row in range(MP):

        def add(i, sums):
            d = i * MP + row
            before = groups[row, jnp.maximum(i - 1, 0)]
            lead = (groups[row, i] != before).astype(jnp.float32)
            keep = 1.0 - lead
            c = d // SETS
            q = d % SETS
            out = []
            for t in range(2):
                inv = 1.0 / scale_send[d, pl.ds(t, 1), :]
                v = x[t, q, :, pl.ds(pl.multiple_of(c * BLK, BLK), BLK)]
                v = (v * inv).astype(jnp.bfloat16).astype(jnp.float32)
                send_p[d, t] = (sums[t] * lead).astype(jnp.bfloat16)
                out.append(sums[t] * keep + v)
            return tuple(out)

        zero = jnp.zeros((ROWS, BLK), jnp.float32)
        last = lax.fori_loop(0, FS, add, (zero, zero))
        for t in range(2):
            send_p[row, t] = last[t].astype(jnp.bfloat16)

    send_all(send_p, recv_p, ps_sem, pr_sem)
    recv_p[f, m] = send_p[me]

    wait_all(scale_recv, sr_sem, FS - 1)
    eye = lax.broadcasted_iota(jnp.int32, (FS, BLK), 0) == lax.broadcasted_iota(
        jnp.int32, (FS, BLK), 1
    )
    for t in range(2):
        came = scale_recv[:, t, :]
        scales[t] = jnp.sum(jnp.where(eye, came, 0.0), axis=0, keepdims=True)[:, :FS]

    quants = (first_quant, second_quant)

    wait_all(send_q, qr_sem, N - 1)

    def finish(k, carry):
        for t in range(2):
            inv = 1.0 / scale_recv[k, pl.ds(t, 1), :]
            for r in range(MP):
                v = recv_q[k, r, t].astype(jnp.float32)
                quants[t][k, r * ROWS : (r + 1) * ROWS, :] = (v * inv).astype(jnp.bfloat16)
        return carry

    lax.fori_loop(0, FS, finish, 0)

    wait_all(send_q, qs_sem, N - 1)
    wait_all(scale_send, ss_sem, FS - 1)
    wait_all(peak_recv, ks_sem, MP - 1)
    wait_all(send_p, ps_sem, N - 1)
    wait_all(send_p, pr_sem, N - 1)


def write(q1, q2, sc, sums, first_quant, second_quant, first_scale, second_scale, parity, wide, sem, wide_sem):
    copies = [
        pltpu.make_async_copy(q1, first_quant, sem.at[0]),
        pltpu.make_async_copy(q2, second_quant, sem.at[1]),
        pltpu.make_async_copy(sc.at[0], first_scale, sem.at[2]),
        pltpu.make_async_copy(sc.at[1], second_scale, sem.at[3]),
    ]
    for copy in copies:
        copy.start()
    w = FS // PARTS
    for b in range(PARTS):

        def widen(k, carry):
            for t in range(2):
                for r in range(MP):
                    wide[t, k, r * ROWS : (r + 1) * ROWS, :] = sums[k, r, t].astype(jnp.float32)
            return carry

        lax.fori_loop(b * w, (b + 1) * w, widen, 0)
        for t in range(2):
            part = pl.ds(b * w, w)
            copy = pltpu.make_async_copy(wide.at[t, part], parity.at[t, part], wide_sem.at[t, b])
            copy.start()
            copies.append(copy)
    for copy in copies:
        copy.wait()


def shards(first_moment, second_moment, parity_groups):
    hbm = pl.BlockSpec(memory_space=pltpu.HBM)
    vmem = pl.BlockSpec(memory_space=pltpu.VMEM)
    dma = pltpu.SemaphoreType.DMA
    f32, bf16 = jnp.float32, jnp.bfloat16
    in_hbm = lambda a: pltpu.with_memory_space_constraint(a, pltpu.HBM)
    results = pl.pallas_call(
        kernel,
        out_shape=(
            jax.ShapeDtypeStruct((FS, BLK, BLK), bf16),
            jax.ShapeDtypeStruct((FS, BLK, BLK), bf16),
            jax.ShapeDtypeStruct((2, 1, FS), f32),
            jax.ShapeDtypeStruct((FS, MP, 2, ROWS, BLK), bf16),
        ),
        in_specs=[hbm, hbm, hbm],
        out_specs=(vmem, vmem, vmem, vmem),
        scratch_shapes=[
            pltpu.SMEM((MP, FS), jnp.int32),
            pltpu.VMEM((2, SETS, ROWS, COLS * BLK), f32),
            pltpu.VMEM((N, 2, ROWS, BLK), bf16),
            pltpu.VMEM((N, 2, ROWS, BLK), bf16),
            pltpu.VMEM((FS, MP, 2, ROWS, BLK), bf16),
            pltpu.VMEM((2, N, 8, BLK), f32),
            pltpu.VMEM((2, N), f32),
            pltpu.VMEM((MP, 2, N), f32),
            pltpu.VMEM((N, 2, BLK), f32),
            pltpu.VMEM((FS, 2, BLK), f32),
            dma((2 * CHUNKS,)), dma,
            dma, dma,
            dma, dma,
            dma, dma,
            dma, dma,
        ],
        compiler_params=pltpu.CompilerParams(
            collective_id=0, has_side_effects=True, vmem_limit_bytes=24 << 20
        ),
        name="relayout",
    )(
        in_hbm(parity_groups),
        in_hbm(first_moment.reshape(SETS, ROWS, COLS * BLK)),
        in_hbm(second_moment.reshape(SETS, ROWS, COLS * BLK)),
    )
    fq, sq, fs, ss, par = pl.pallas_call(
        write,
        out_shape=(
            jax.ShapeDtypeStruct((FS, BLK, BLK), bf16),
            jax.ShapeDtypeStruct((FS, BLK, BLK), bf16),
            jax.ShapeDtypeStruct((1, FS), f32),
            jax.ShapeDtypeStruct((1, FS), f32),
            jax.ShapeDtypeStruct((2, FS, BLK, BLK), f32),
        ),
        in_specs=[vmem] * 4,
        out_specs=(hbm,) * 5,
        scratch_shapes=[pltpu.VMEM((2, FS, BLK, BLK), f32), dma((4,)), dma((2, PARTS))],
        compiler_params=pltpu.CompilerParams(vmem_limit_bytes=8 << 20),
        name="write",
    )(*results)
    return fq[None], sq[None], fs, ss, par.reshape(1, 2, 1, FS, BLK, BLK)


def solution(mesh):
    in_specs = (P(None, None, "fsdp", "mp", None), P(None, None, "fsdp", "mp", None), P())
    out_specs = (
        P(None, ("fsdp", "mp"), None, None),
        P(None, ("fsdp", "mp"), None, None),
        P(None, ("fsdp", "mp")),
        P(None, ("fsdp", "mp")),
        P(("fsdp", "mp"), None, None, None, None, None),
    )
    return jax.shard_map(shards, mesh=mesh, in_specs=in_specs, out_specs=out_specs, check_vma=False)
```

time: 72.7 us -> 62.1 us (0.85)
  local copies, waits for them, and re-layouts: 8.83 us -> 0 us
  Pallas kernels: 63 us -> 61.4 us
    unnamed x11 -> x0, local copies, waits for them, and re-layouts: 8.83 us -> none
    pallas_call x1, Pallas kernels: 63 us -> 58.6 us  [shards(): pl.pallas_call(kernel, out_shape=(jax.ShapeDtypeStruct((FS, BLK, BLK), bf...]
    pallas_call x0 -> x1, Pallas kernels: none -> 2.82 us  [shards(): pl.pallas_call(write, out_shape=(jax.ShapeDtypeStruct((FS, BLK, BLK), bf1...]
where the time goes in v2:
time: 62.1 us; the launch traced here: 62 us
  Pallas kernels  61.4 us (99%)
  between operations  0.64 us (1%)
    pallas_call x1, Pallas kernels, shards(): pl.pallas_call(kernel, out_shape=(jax.ShapeDtypeStruct((FS, BLK, BLK), bf...  58.6 us
    pallas_call x1, Pallas kernels, shards(): pl.pallas_call(write, out_shape=(jax.ShapeDtypeStruct((FS, BLK, BLK), bf1...  2.82 us

profile of v2, /device:TPU:1, one launch (start us, length us, event | category | flops | bytes accessed | tf_op | source)
XLA Modules:
  0.0 62.0 jit_solution(4109971329242603147)
XLA Ops:
  0.6 58.6 %relayout.1 = (bf16[32,128,128]{2,1,0:T(8,128)(2,1)S(1)}, bf16[32,128,128]{2,1,0:T(8,128)(2,1)S(1)}, f32[2,1,32]{2,1,0:T(1,128)S(1)}, bf16[32,4,2,32,128]{4,3,2,1,0:T(8,128)(2,1)S(1)}) custom-call(s32[4,32]{1,0:T(4,128)} %groups_in.1, f32[16,32,1024]{2,1,0:T(8,128)} %bitcast.7, f32[16,32,1024]{2,1,0:T(8,128)} %bitcast.8), custom_call_target="tpu_custom_call" | custom-call | tf_op jit(solution)/shard_map/relayout/pallas_call | solution.py:219
  59.2 2.8 %write.1 = (bf16[32,128,128]{2,1,0:T(8,128)(2,1)}, bf16[32,128,128]{2,1,0:T(8,128)(2,1)}, f32[1,32]{1,0:T(1,128)}, f32[1,32]{1,0:T(1,128)}, f32[2,32,128,128]{3,2,1,0:T(8,128)}) custom-call(bf16[32,128,128]{2,1,0:T(8,128)(2,1)S(1)} %get-tuple-element.14.q1, bf16[32,128,128]{2,1,0:T(8,128)(2,1)S(1)} %get-tuple-element.15.q2, ...), custom_call_target="tpu_custom_call" | custom-call | tf_op jit(solution)/shard_map/write/pallas_call | solution.py:255

commit v3 on v2

--- a/solution.py
+++ b/solution.py
@@ -13,8 +13,10 @@
 ROWS = BLK // MP
 COLS = 8
 SETS = 16
-CHUNKS = 4
+BAND = 4
+DY = (0, 1, 3, 2)
 PARTS = 8
+ROUNDS = 5
 epsilon = 1e-06
 
 def distance(step):
@@ -25,6 +27,8 @@
     (i // 32, (i // 8) % 4, (i // 2) % 4, i % 2) for i in ((n * 53) % N for n in range(1, N))
 ]
 STEPS.sort(key=lambda step: -distance(step))
+SHELLS = [[step for step in STEPS if distance(step) == r] for r in range(7)]
+NEAR = SHELLS[0] + SHELLS[1]
 
 
 def target(f, m, step):
@@ -45,7 +49,7 @@
     first_quant, second_quant, scales, recv_p,
     groups, x, send_q, send_p, recv_q,
     partial, peak_send, peak_recv, scale_send, scale_recv,
-    in_sem, g_sem, qs_sem, qr_sem, ps_sem, pr_sem, ks_sem, kr_sem, ss_sem, sr_sem,
+    in_sem, g_sem, qs_sem, qr_sem, ps_sem, pr_sem, ks_sem, kr_sem, ss_sem, sr_sem, round_sem,
 ):
     f = lax.axis_index("fsdp")
     m = lax.axis_index("mp")
@@ -55,56 +59,85 @@
 
     groups_load = pltpu.make_async_copy(groups_in, groups, g_sem)
     groups_load.start()
-    loads = []
-    for t, ref in enumerate((first, second)):
-        for b in range(CHUNKS):
-            w = SETS // CHUNKS
-            load = pltpu.make_async_copy(
-                ref.at[pl.ds(b * w, w)], x.at[t, pl.ds(b * w, w)], in_sem.at[t * CHUNKS + b]
+    def near_y(dy):
+        return (f % 4 + dy) % 4 * BAND
+
+    loads = {}
+    for n, dy in enumerate(DY):
+        rows = pl.ds(near_y(dy), BAND)
+        for t, ref in enumerate((first, second)):
+            loads[dy, t] = pltpu.make_async_copy(ref.at[rows], x.at[t, rows], in_sem.at[n * 2 + t])
+            loads[dy, t].start()
+
+    def tell(sem):
+        for step in NEAR:
+            pl.semaphore_signal(
+                sem, inc=1, device_id=target(f, m, step), device_id_type=LOGICAL
             )
-            load.start()
-            loads.append(load)
-
-    others = [target(f, m, step) for step in STEPS]
-    for other in others:
-        pl.semaphore_signal(barrier, inc=1, device_id=other, device_id_type=LOGICAL)
-
-    for t in range(2):
-        for b in range(CHUNKS):
-            loads[t * CHUNKS + b].wait()
-            w = SETS // CHUNKS
-
-            def cast(q, carry):
+
+    tell(barrier)
+
+    def send(src, dst, s_sem, r_sem, steps):
+        for step in steps:
+            other = target(f, m, step)
+            pltpu.make_async_remote_copy(
+                src_ref=src.at[other], dst_ref=dst.at[f, m], send_sem=s_sem, recv_sem=r_sem,
+                device_id=other, device_id_type=LOGICAL,
+            ).start()
+
+    def heard(r):
+        pl.semaphore_wait(barrier if r == 0 else round_sem.at[r - 1], len(NEAR))
+        if r < ROUNDS:
+            tell(round_sem.at[r])
+
+    def cast(dy):
+        for t in range(2):
+            loads[dy, t].wait()
+        base = near_y(dy)
+
+        def one(i, carry):
+            q = base + i
+            for t in range(2):
                 for c in range(COLS):
                     v = x[t, q, :, c * BLK : (c + 1) * BLK]
                     send_q[c * SETS + q, t] = v.astype(jnp.bfloat16)
                     a = jnp.abs(v)
-                    a = jnp.maximum(
+                    partial[t, c * SETS + q] = jnp.maximum(
                         jnp.maximum(a[0:8], a[8:16]), jnp.maximum(a[16:24], a[24:32])
                     )
-                    partial[t, c * SETS + q] = a
-                return carry
-
-            lax.fori_loop(b * w, (b + 1) * w, cast, 0)
+            return carry
+
+        lax.fori_loop(0, BAND, one, 0)
+
+    def send_q_part(radii, dys):
+        steps = [step for r in radii for step in SHELLS[r] if step[2] in dys]
+        send(send_q, recv_q, qs_sem, qr_sem, steps)
+
+    cast(0)
+    cast(1)
+    heard(0)
+    send_q_part((0, 1), (0, 1))
+    cast(3)
+    heard(1)
+    send_q_part((2,), (0, 1))
+    cast(2)
+    send_q_part((1, 2), (3,))
+    heard(2)
+    send_q_part((2,), (2,))
+
+    for t in range(2):
         rows = jnp.max(partial[t], axis=1)
         peak_send[t : t + 1, :] = jnp.max(rows.T, axis=0, keepdims=True)
-
-    pl.semaphore_wait(barrier, N - 1)
-
     for k in range(1, MP):
         pltpu.make_async_remote_copy(
             src_ref=peak_send, dst_ref=peak_recv.at[m], send_sem=ks_sem, recv_sem=kr_sem,
             device_id=f * MP + (m + k) % MP, device_id_type=LOGICAL,
         ).start()
 
-    def send_all(src, dst, s_sem, r_sem):
-        for other in others:
-            pltpu.make_async_remote_copy(
-                src_ref=src.at[other], dst_ref=dst.at[f, m], send_sem=s_sem, recv_sem=r_sem,
-                device_id=other, device_id_type=LOGICAL,
-            ).start()
-
-    send_all(send_q, recv_q, qs_sem, qr_sem)
+    send(send_q, recv_q, qs_sem, qr_sem, SHELLS[3])
+    for r in range(3, ROUNDS + 1):
+        heard(r)
+        send(send_q, recv_q, qs_sem, qr_sem, SHELLS[r + 1])
     recv_q[f, m] = send_q[me]
 
     peak_recv[m] = peak_send[...]
@@ -150,7 +183,7 @@
         for t in range(2):
             send_p[row, t] = last[t].astype(jnp.bfloat16)
 
-    send_all(send_p, recv_p, ps_sem, pr_sem)
+    send(send_p, recv_p, ps_sem, pr_sem, STEPS)
     recv_p[f, m] = send_p[me]
 
     wait_all(scale_recv, sr_sem, FS - 1)
@@ -237,11 +270,12 @@
             pltpu.VMEM((MP, 2, N), f32),
             pltpu.VMEM((N, 2, BLK), f32),
             pltpu.VMEM((FS, 2, BLK), f32),
-            dma((2 * CHUNKS,)), dma,
+            dma((2 * len(DY),)), dma,
             dma, dma,
             dma, dma,
             dma, dma,
             dma, dma,
+            pltpu.SemaphoreType.REGULAR((ROUNDS,)),
         ],
         compiler_params=pltpu.CompilerParams(
             collective_id=0, has_side_effects=True, vmem_limit_bytes=24 << 20

time: 62.1 us -> 60.8 us (0.979)
  Pallas kernels: 61.4 us -> 60.1 us
    pallas_call x1, Pallas kernels: 58.6 us -> 57.3 us  [shards(): pl.pallas_call(kernel, out_shape=(jax.ShapeDtypeStruct((FS, BLK, BLK), bf...]
where the time goes in v3:
time: 60.8 us; the launch traced here: 60.7 us
  Pallas kernels  60.1 us (99%)
  between operations  0.64 us (1%)
    pallas_call x1, Pallas kernels, shards(): pl.pallas_call(kernel, out_shape=(jax.ShapeDtypeStruct((FS, BLK, BLK), bf...  57.3 us
    pallas_call x1, Pallas kernels, shards(): pl.pallas_call(write, out_shape=(jax.ShapeDtypeStruct((FS, BLK, BLK), bf1...  2.82 us

profile of v3, /device:TPU:1, one launch (start us, length us, event | category | flops | bytes accessed | tf_op | source)
XLA Modules:
  0.0 60.7 jit_solution(16661818398966817698)
XLA Ops:
  0.6 57.3 %relayout.1 = (bf16[32,128,128]{2,1,0:T(8,128)(2,1)S(1)}, bf16[32,128,128]{2,1,0:T(8,128)(2,1)S(1)}, f32[2,1,32]{2,1,0:T(1,128)S(1)}, bf16[32,4,2,32,128]{4,3,2,1,0:T(8,128)(2,1)S(1)}) custom-call(s32[4,32]{1,0:T(4,128)} %groups_in.1, f32[16,32,1024]{2,1,0:T(8,128)} %bitcast.7, f32[16,32,1024]{2,1,0:T(8,128)} %bitcast.8), custom_call_target="tpu_custom_call" | custom-call | tf_op jit(solution)/shard_map/relayout/pallas_call | solution.py:252
  57.9 2.8 %write.1 = (bf16[32,128,128]{2,1,0:T(8,128)(2,1)}, bf16[32,128,128]{2,1,0:T(8,128)(2,1)}, f32[1,32]{1,0:T(1,128)}, f32[1,32]{1,0:T(1,128)}, f32[2,32,128,128]{3,2,1,0:T(8,128)}) custom-call(bf16[32,128,128]{2,1,0:T(8,128)(2,1)S(1)} %get-tuple-element.14.q1, bf16[32,128,128]{2,1,0:T(8,128)(2,1)S(1)} %get-tuple-element.15.q2, ...), custom_call_target="tpu_custom_call" | custom-call | tf_op jit(solution)/shard_map/write/pallas_call | solution.py:289

commit v4 on v3

--- a/solution.py
+++ b/solution.py
@@ -28,6 +28,7 @@
 ]
 STEPS.sort(key=lambda step: -distance(step))
 SHELLS = [[step for step in STEPS if distance(step) == r] for r in range(7)]
+SUMS = sorted([(i // 32, (i // 8) % 4, (i // 2) % 4, i % 2) for i in ((n * 107) % N for n in range(1, N))], key=lambda step: -distance(step))
 NEAR = SHELLS[0] + SHELLS[1]
 
 
@@ -183,7 +184,7 @@
         for t in range(2):
             send_p[row, t] = last[t].astype(jnp.bfloat16)
 
-    send(send_p, recv_p, ps_sem, pr_sem, STEPS)
+    send(send_p, recv_p, ps_sem, pr_sem, SUMS)
     recv_p[f, m] = send_p[me]
 
     wait_all(scale_recv, sr_sem, FS - 1)

time: 60.8 us -> 60.8 us (level)
  no operation moved by 1% of the time
where the time goes in v4:
time: 60.8 us; the launch traced here: 60.7 us
  Pallas kernels  60.1 us (99%)
  between operations  0.64 us (1%)
    pallas_call x1, Pallas kernels, shards(): pl.pallas_call(kernel, out_shape=(jax.ShapeDtypeStruct((FS, BLK, BLK), bf...  57.3 us
    pallas_call x1, Pallas kernels, shards(): pl.pallas_call(write, out_shape=(jax.ShapeDtypeStruct((FS, BLK, BLK), bf1...  2.82 us

profile of v4, /device:TPU:1, one launch (start us, length us, event | category | flops | bytes accessed | tf_op | source)
XLA Modules:
  0.0 60.7 jit_solution(13824192945353289629)
XLA Ops:
  0.6 57.3 %relayout.1 = (bf16[32,128,128]{2,1,0:T(8,128)(2,1)S(1)}, bf16[32,128,128]{2,1,0:T(8,128)(2,1)S(1)}, f32[2,1,32]{2,1,0:T(1,128)S(1)}, bf16[32,4,2,32,128]{4,3,2,1,0:T(8,128)(2,1)S(1)}) custom-call(s32[4,32]{1,0:T(4,128)} %groups_in.1, f32[16,32,1024]{2,1,0:T(8,128)} %bitcast.7, f32[16,32,1024]{2,1,0:T(8,128)} %bitcast.8), custom_call_target="tpu_custom_call" | custom-call | tf_op jit(solution)/shard_map/relayout/pallas_call | solution.py:253
  57.9 2.8 %write.1 = (bf16[32,128,128]{2,1,0:T(8,128)(2,1)}, bf16[32,128,128]{2,1,0:T(8,128)(2,1)}, f32[1,32]{1,0:T(1,128)}, f32[1,32]{1,0:T(1,128)}, f32[2,32,128,128]{3,2,1,0:T(8,128)}) custom-call(bf16[32,128,128]{2,1,0:T(8,128)(2,1)S(1)} %get-tuple-element.14.q1, bf16[32,128,128]{2,1,0:T(8,128)(2,1)S(1)} %get-tuple-element.15.q2, ...), custom_call_target="tpu_custom_call" | custom-call | tf_op jit(solution)/shard_map/write/pallas_call | solution.py:290
